TPU v7x, 32 devices: a whole 2x2x4 slice. The times are simulated.
32 devices in a mesh: shard: 2 (over core), cols: 4 (over y, x), job: 4 (over z).
Axes of the slice: x: 2, y: 2, z: 4, core: 2. Of those that a mesh axis runs over, the one named last changes fastest.
Arguments:
- one_query: float32 [16384, 4096], P(('job', 'shard'), 'cols'), parts along dimension 0, may hold values from -0.125 to 0.125
- other_query: float32 [16384, 4096], P(('job', 'shard'), 'cols'), parts along dimension 0, may hold values from -0.09375 to 0.09375
- one_key: float32 [16384, 1024], P(('job', 'shard'), 'cols'), parts along dimension 0, may hold values from -0.125 to 0.125
- other_key: float32 [16384, 1024], P(('job', 'shard'), 'cols'), parts along dimension 0, may hold values from -0.09375 to 0.09375
- one_value: float32 [16384, 1024], P(('job', 'shard'), 'cols'), parts along dimension 0, may hold values from -0.125 to 0.125
- other_value: float32 [16384, 1024], P(('job', 'shard'), 'cols'), parts along dimension 0, may hold values from -0.09375 to 0.09375
- mix_share: float32 [16384], P(('job', 'shard')), parts along dimension 0, may hold values from 0.2 to 0.8
- norm_gain: float32 [16384], P(('job', 'shard')), parts along dimension 0, may hold values from 0.25 to 1.75
Outputs:
- final_query: bfloat16 [16384, 4096], P('job', 'cols'), parts along dimension 0
- final_key: bfloat16 [16384, 1024], P('job', 'cols'), parts along dimension 0
- final_value: bfloat16 [16384, 1024], P('job', 'cols'), parts along dimension 0
- scale_query: float32 [16384], P(('job', 'cols')), parts along dimension 0
- scale_key: float32 [4096], P(('job', 'cols')), parts along dimension 0
- scale_value: float32 [4096], P(('job', 'cols')), parts along dimension 0
There are 4 independent parts, one for each index of `job`. A program takes and returns all parts, laid end to end along the dimension named above; each array names one. Nothing has to cross between parts.
All inputs are finite; a program needn't handle non-finite values. Where the computation divides by a largest or mean magnitude, that divisor is 1e-20 or more.
Results may differ from a plain program's by a relative error of at most 0.001.
Values may be sent and summed in bfloat16 or wider, within the bound.
A program may use at most 128 MiB of HBM per device.

v0:
```python
import jax
import jax.numpy as jnp
from jax import lax
from jax.sharding import PartitionSpec as P


def shards(
    one_query, other_query, one_key, other_key, one_value, other_value, mix_share, norm_gain
):
    result_query = mix_share[:, None] * one_query + (1.0 - mix_share[:, None]) * other_query
    result_key = mix_share[:, None] * one_key + (1.0 - mix_share[:, None]) * other_key
    result_value = mix_share[:, None] * one_value + (1.0 - mix_share[:, None]) * other_value
    result_gained_query = result_query * norm_gain[:, None]
    result_gained_key = result_key * norm_gain[:, None]
    result_gained_value = result_value * norm_gain[:, None]
    scale_query, scale_key, scale_value = lax.pmax(
        (
            jnp.max(jnp.abs(result_gained_query), axis=0),
            jnp.max(jnp.abs(result_gained_key), axis=0),
            jnp.max(jnp.abs(result_gained_value), axis=0),
        ),
        "shard",
    )
    narrow_query, narrow_key, narrow_value = (
        (result_gained_query / scale_query).astype(jnp.bfloat16),
        (result_gained_key / scale_key).astype(jnp.bfloat16),
        (result_gained_value / scale_value).astype(jnp.bfloat16),
    )
    final_query, final_key, final_value = (
        lax.all_gather(narrow_query, "shard", axis=0, tiled=True),
        lax.all_gather(narrow_key, "shard", axis=0, tiled=True),
        lax.all_gather(narrow_value, "shard", axis=0, tiled=True),
    )
    return (final_query, final_key, final_value, scale_query, scale_key, scale_value)


def solution(mesh):
    placed = (
        P(("job", "shard"), "cols"),
        P(("job", "shard"), "cols"),
        P(("job", "shard"), "cols"),
        P(("job", "shard"), "cols"),
        P(("job", "shard"), "cols"),
        P(("job", "shard"), "cols"),
        P(("job", "shard")),
        P(("job", "shard")),
    )
    return jax.shard_map(
        shards,
        mesh=mesh,
        in_specs=placed,
        out_specs=(
            P("job", "cols"),
            P("job", "cols"),
            P("job", "cols"),
            P(("job", "cols")),
            P(("job", "cols")),
            P(("job", "cols")),
        ),
        check_vma=False,
    )
```

profile of v0, /device:TPU:3, one launch (start us, length us, event | category | flops | bytes accessed | tf_op | source)
XLA Modules:
  0.0 93.3 jit_solution(1859230134611936218)
XLA Ops:
  7.2 0.0 all-gather.6.cloned.1.call-start
  7.2 0.7 broadcast_subtract_fusion
  7.9 0.0 copy-start.2
  7.9 0.0 copy-start.3
  7.9 0.0 copy-start.4
  7.9 0.0 copy-start.5
  7.9 0.0 copy-start.6
  7.9 0.0 copy-start.7
  8.0 10.3 %abs_reduce_fusion = (f32[1024]{0:T(1024)S(1)}, f32[2048,1024]{1,0:T(8,128)}) fusion(f32[2048]{0:T(1024)} %param.15, f32[2048,1024]{1,0:T(8,128)} %param.9, f32[2048]{0:T(1024)S(1)} %broadcast_subtract_fusion, f32[2048,1024]{1,0:T(8,128)} %param.8, f32[2048]{0:T(1024)} %param.14), kind=kLoop, calls=%fused_computation.1 | loop fusion | flops 12581888 | bytes 25194496 | tf_op jit(solution)/shard_map/reduce_max | solution.py:18
  18.3 0.0 copy-done.2
  18.3 0.0 copy-done.3
  18.3 0.0 copy-done.4
  18.3 0.7 copy-done.5
  19.0 0.0 copy-done.6
  19.0 0.0 copy-done.7
  19.0 1.9 %abs_reduce_fusion.1 = (f32[256]{0:T(256)S(1)}, f32[2048,256]{1,0:T(8,128)S(1)}, f32[256]{0:T(256)S(1)}, f32[2048,256]{1,0:T(8,128)}) fusion(f32[2048]{0:T(1024)S(1)} %copy-done.7, f32[2048,256]{1,0:T(8,128)S(1)} %copy-done.2, f32[2048]{0:T(1024)S(1)} %broadcast_subtract_fusion, f32[2048,256]{1,0:T(8,128)S(1)} %copy-done.3, f32[2048]{0:T(1024)S(1)} %copy-done.6, ...), kind=kLoop, calls=%fused_computation.4 | loop fusion | flops 6290944 | bytes 12609536 | tf_op jit(solution)/shard_map/reduce_max | solution.py:20
  21.0 2.8 %all-reduce = (f32[1024]{0:T(1024)S(1)}, f32[256]{0:T(256)S(1)}, f32[256]{0:T(256)S(1)}) all-reduce(f32[1024]{0:T(1024)S(1)} %get-tuple-element.13, f32[256]{0:T(256)S(1)} %get-tuple-element.15, f32[256]{0:T(256)S(1)} %get-tuple-element.9), channel_id=1, replica_groups=mesh['shard'=2,'cols'=4,'job'=4] {'shard'}, use_global_device_ids=true, to_apply=%region_1.0 | all-reduce | flops 1536 | bytes 12288 | tf_op jit(solution)/shard_map/pmax | solution.py:16
  23.8 0.0 copy-start.9
  23.8 0.0 copy-start.10
  23.8 0.0 copy-start.8
  23.8 2.7 %divide_convert_fusion.2 = bf16[2048,256]{1,0:T(8,128)(2,1)} fusion(f32[2048,256]{1,0:T(8,128)} %get-tuple-element.16, f32[256]{0:T(256)S(1)} %get-tuple-element.27), kind=kLoop, calls=%fused_computation.6 | loop fusion | flops 1048576 | bytes 3146752 | tf_op jit(solution)/shard_map/convert_element_type | solution.py:26
  26.5 0.0 all-gather.6.cloned.1.call-update
  26.5 0.0 copy-done.9
  26.5 0.0 all-gather.8.cloned.1.call-start
  26.6 0.0 copy-done.10
  26.6 1.1 %divide_convert_fusion.1 = bf16[2048,256]{1,0:T(8,128)(2,1)} fusion(f32[2048,256]{1,0:T(8,128)S(1)} %get-tuple-element.10, f32[256]{0:T(256)S(1)} %get-tuple-element.28), kind=kLoop, calls=%fused_computation.3 | loop fusion | flops 1048576 | bytes 3146752 | tf_op jit(solution)/shard_map/convert_element_type | solution.py:27
  27.7 0.0 all-gather.8.cloned.1.call-update
  27.8 0.0 all-gather.4.cloned.1.call-start
  27.8 0.0 copy-done.8
  27.8 6.6 %divide_convert_fusion = bf16[2048,1024]{1,0:T(8,128)(2,1)} fusion(f32[2048,1024]{1,0:T(8,128)} %get-tuple-element.14, f32[1024]{0:T(1024)S(1)} %get-tuple-element.26), kind=kLoop, calls=%fused_computation | loop fusion | flops 4194304 | bytes 12587008 | tf_op jit(solution)/shard_map/convert_element_type | solution.py:25
  34.4 0.0 all-gather.4.cloned.1.call-update
  34.5 4.4 %all-gather.6.cloned.1.call-done = bf16[4096,256]{1,0:T(8,128)(2,1)} async-done(((bf16[2048,256]{1,0:T(8,128)(2,1)}), bf16[4096,256]{1,0:T(8,128)(2,1)}) %all-gather.6.cloned.1.call-update) | async-done | bytes 2097168 | tf_op jit(solution)/shard_map/all_gather | solution.py:31
  38.9 0.0 copy-start
  38.9 13.9 %all-gather.8.cloned.1.call-done = bf16[4096,256]{1,0:T(8,128)(2,1)} async-done(((bf16[2048,256]{1,0:T(8,128)(2,1)}), bf16[4096,256]{1,0:T(8,128)(2,1)}) %all-gather.8.cloned.1.call-update) | async-done | bytes 2097168 | tf_op jit(solution)/shard_map/all_gather | solution.py:32
  52.8 22.6 %all-gather.4.cloned.1.call-done = bf16[4096,1024]{1,0:T(8,128)(2,1)} async-done(((bf16[2048,1024]{1,0:T(8,128)(2,1)}), bf16[4096,1024]{1,0:T(8,128)(2,1)}) %all-gather.4.cloned.1.call-update) | async-done | bytes 8388624 | tf_op jit(solution)/shard_map/all_gather | solution.py:30
  75.4 7.8 %copy.17 = bf16[4096,1024]{1,0:T(8,128)(2,1)} copy(bf16[4096,1024]{1,0:T(8,128)(2,1)} %all-gather.4.cloned.1.call-done) | data formatting | bytes 16777216
  83.1 0.0 copy-done
  83.1 0.0 copy-start.1
  83.1 1.3 %copy.18 = bf16[4096,256]{1,0:T(8,128)(2,1)} copy(bf16[4096,256]{1,0:T(8,128)(2,1)S(1)} %copy-done) | data formatting | bytes 4194304
  84.5 1.0 %copy-done.1 = bf16[4096,256]{1,0:T(8,128)(2,1)S(1)} copy-done((bf16[4096,256]{1,0:T(8,128)(2,1)S(1)}, bf16[4096,256]{1,0:T(8,128)(2,1)}, u32[]{:S(2)}) %copy-start.1) | copy-done | bytes 2097176
  85.5 1.3 %copy.19 = bf16[4096,256]{1,0:T(8,128)(2,1)} copy(bf16[4096,256]{1,0:T(8,128)(2,1)S(1)} %copy-done.1) | data formatting | bytes 4194304
Async XLA Ops:
  7.2 31.7 %all-gather.6.cloned.1.call-start = ((), (), s32[]{:S(2)}) async-start(), calls=%async_computation.1 | async-start | bytes 3145728 | tf_op jit(solution)/shard_map/all_gather | solution.py:31
  7.9 10.4 %copy-start.2 = (f32[2048,256]{1,0:T(8,128)S(1)}, f32[2048,256]{1,0:T(8,128)}, u32[]{:S(2)}) copy-start(f32[2048,256]{1,0:T(8,128)} %param.13) | copy-start | bytes 6291460
  7.9 10.4 %copy-start.3 = (f32[2048,256]{1,0:T(8,128)S(1)}, f32[2048,256]{1,0:T(8,128)}, u32[]{:S(2)}) copy-start(f32[2048,256]{1,0:T(8,128)} %param.12) | copy-start | bytes 6291460
  7.9 10.4 %copy-start.4 = (f32[2048,256]{1,0:T(8,128)S(1)}, f32[2048,256]{1,0:T(8,128)}, u32[]{:S(2)}) copy-start(f32[2048,256]{1,0:T(8,128)} %param.11) | copy-start | bytes 6291460
  7.9 11.1 %copy-start.5 = (f32[2048,256]{1,0:T(8,128)S(1)}, f32[2048,256]{1,0:T(8,128)}, u32[]{:S(2)}) copy-start(f32[2048,256]{1,0:T(8,128)} %param.10) | copy-start | bytes 6291460
  7.9 11.1 %copy-start.6 = (f32[2048]{0:T(1024)S(1)}, f32[2048]{0:T(1024)}, u32[]{:S(2)}) copy-start(f32[2048]{0:T(1024)} %param.14) | copy-start | bytes 24580
  7.9 11.1 %copy-start.7 = (f32[2048]{0:T(1024)S(1)}, f32[2048]{0:T(1024)}, u32[]{:S(2)}) copy-start(f32[2048]{0:T(1024)} %param.15) | copy-start | bytes 24580
  23.8 2.8 %copy-start.9 = (f32[256]{0:T(256)}, f32[256]{0:T(256)S(1)}, u32[]{:S(2)}) copy-start(f32[256]{0:T(256)S(1)} %get-tuple-element.27) | copy-start | bytes 3076
  23.8 2.8 %copy-start.10 = (f32[256]{0:T(256)}, f32[256]{0:T(256)S(1)}, u32[]{:S(2)}) copy-start(f32[256]{0:T(256)S(1)} %get-tuple-element.28) | copy-start | bytes 3076
  23.8 4.0 %copy-start.8 = (f32[1024]{0:T(1024)}, f32[1024]{0:T(1024)S(1)}, u32[]{:S(2)}) copy-start(f32[1024]{0:T(1024)S(1)} %get-tuple-element.26) | copy-start | bytes 12292
  26.5 26.2 %all-gather.8.cloned.1.call-start = ((), (), s32[]{:S(2)}) async-start(), calls=%async_computation.2 | async-start | bytes 3145728 | tf_op jit(solution)/shard_map/all_gather | solution.py:32
  27.8 47.6 %all-gather.4.cloned.1.call-start = ((), (), s32[]{:S(2)}) async-start(), calls=%async_computation | async-start | bytes 12582912 | tf_op jit(solution)/shard_map/all_gather | solution.py:30
  38.9 44.3 %copy-start = (bf16[4096,256]{1,0:T(8,128)(2,1)S(1)}, bf16[4096,256]{1,0:T(8,128)(2,1)}, u32[]{:S(2)}) copy-start(bf16[4096,256]{1,0:T(8,128)(2,1)} %all-gather.6.cloned.1.call-done) | copy-start | bytes 6291460
  83.1 2.3 %copy-start.1 = (bf16[4096,256]{1,0:T(8,128)(2,1)S(1)}, bf16[4096,256]{1,0:T(8,128)(2,1)}, u32[]{:S(2)}) copy-start(bf16[4096,256]{1,0:T(8,128)(2,1)} %all-gather.8.cloned.1.call-done) | copy-start | bytes 6291460
Sparse Core Ops, SparseCore 0:
  26.6 12.1 all-gather.5
  41.0 11.7 all-gather.7
  54.3 21.0 all-gather.3
where the time goes:
time: 94.4 us; the launch traced here: 93.3 us
  waiting for transfers between devices  41 us (43%)
  other arithmetic  23.5 us (25%)
  between operations  13.8 us (15%)
  local copies, waits for them, and re-layouts  12.2 us (13%)
  blocking collectives  2.79 us (3%)
    all_gather x1, waiting for transfers between devices, shards(): lax.all_gather(narrow_query, 'shard', axis=0, tiled=True)  22.6 us
    all_gather x1, waiting for transfers between devices, shards(): lax.all_gather(narrow_value, 'shard', axis=0, tiled=True)  13.9 us
    unnamed x25, local copies, waits for them, and re-layouts  12.2 us
    reduce_max x1, other arithmetic, shards(): jnp.max(jnp.abs(result_gained_query), axis=0)  10.3 us
    convert_element_type x1, other arithmetic, shards(): (result_gained_query / scale_query).astype(jnp.bfloat16)  6.62 us
    all_gather x1, waiting for transfers between devices, shards(): lax.all_gather(narrow_key, 'shard', axis=0, tiled=True)  4.41 us
    pmax x1, blocking collectives, shards(): lax.pmax((jnp.max(jnp.abs(result_gained_query), axis=0), jnp.max(jnp.abs(...  2.79 us
    convert_element_type x1, other arithmetic, shards(): (result_gained_key / scale_key).astype(jnp.bfloat16)  2.73 us
  transfers between devices with their start and end apart: 3, of which 3 were waited for; matrix products, arithmetic and copies ran while one was open for 8% of the time, Pallas kernels for 0%

commit v1 on v0

v1 whole, which is shorter than its diff:
```python
import functools

import jax
import jax.numpy as jnp
from jax import lax
from jax.experimental import pallas as pl
from jax.experimental.pallas import tpu as pltpu
from jax.sharding import PartitionSpec as P

LANES = 128
WIDTH = 128
BLOCK = 128
MESH = pl.DeviceIdType.MESH


def merge(n, chunks, *refs):
    ones, others = refs[0:3], refs[3:6]
    mix_hbm, gain_hbm = refs[6:8]
    finals, scales = refs[8:11], refs[11:14]
    held, extra = refs[14:17], refs[17:20]
    mix_ref, gain_ref, first, second, peaks = refs[20:25]
    row_sem, in_sem, peak_send, peak_recv, send_sem, recv_sem = refs[25:]
    me = lax.axis_index("shard")
    rows = held[0].shape[0]
    peers = [lax.rem(me + k, n) for k in range(1, n)]

    def loads(c):
        a, col = chunks[c]
        cols = pl.ds(col, WIDTH)
        return (
            pltpu.make_async_copy(ones[a].at[:, cols], held[a].at[:, cols], in_sem.at[c, 0]),
            pltpu.make_async_copy(others[a].at[:, cols], extra[a].at[:, cols], in_sem.at[c, 1]),
        )

    def peak_copy(c, k, slot):
        return pltpu.make_async_remote_copy(
            src_ref=peaks.at[c, slot],
            dst_ref=peaks.at[c, slot],
            send_sem=peak_send.at[c, k],
            recv_sem=peak_recv.at[c, slot],
            device_id={"shard": peers[k]},
            device_id_type=MESH,
        )

    def block_copy(c, k, slot):
        a, col = chunks[c]
        block = finals[a].at[pl.ds(pl.multiple_of(slot * rows, rows), rows), pl.ds(col, WIDTH)]
        return pltpu.make_async_remote_copy(
            src_ref=block,
            dst_ref=block,
            send_sem=send_sem.at[c, k],
            recv_sem=recv_sem.at[c, slot],
            device_id={"shard": peers[k]},
            device_id_type=MESH,
        )

    factors = (
        pltpu.make_async_copy(mix_hbm, mix_ref, row_sem.at[0]),
        pltpu.make_async_copy(gain_hbm, gain_ref, row_sem.at[1]),
    )
    for copy in factors:
        copy.start()
    for c in range(len(chunks)):
        for copy in loads(c):
            copy.start()

    barrier = pltpu.get_barrier_semaphore()
    for peer in peers:
        pl.semaphore_signal(barrier, inc=1, device_id={"shard": peer}, device_id_type=MESH)

    for copy in factors:
        copy.wait()
    for k in range(rows // LANES):
        mix = mix_ref[k : k + 1, :]
        gain = gain_ref[k : k + 1, :]
        span = pl.ds(k * LANES, LANES)
        first[span, :] = jnp.broadcast_to(mix * gain, (LANES, LANES)).T
        second[span, :] = jnp.broadcast_to((1.0 - mix) * gain, (LANES, LANES)).T

    pl.semaphore_wait(barrier, n - 1)

    def combine(c):
        a, col = chunks[c]
        for copy in loads(c):
            copy.wait()
        cols = pl.ds(col, WIDTH)

        def step(i, peak):
            span = pl.ds(pl.multiple_of(i * BLOCK, BLOCK), BLOCK)
            value = first[span, :] * held[a][span, cols] + second[span, :] * extra[a][span, cols]
            held[a][span, cols] = value
            return jnp.maximum(peak, jnp.max(jnp.abs(value).reshape(BLOCK // 8, 8, WIDTH), axis=0))

        peaks[c, me] = lax.fori_loop(0, rows // BLOCK, step, jnp.zeros((8, WIDTH), jnp.float32))
        for k in range(n - 1):
            peak_copy(c, k, me).start()

    def finish(c):
        a, col = chunks[c]
        cols = pl.ds(col, WIDTH)
        for k in range(n - 1):
            peak_copy(c, k, peers[k]).wait_recv()
        peak = peaks[c, 0]
        for k in range(1, n):
            peak = jnp.maximum(peak, peaks[c, k])
        scale = jnp.max(peak, axis=0, keepdims=True)
        row = col // LANES
        scales[a][row : row + 1, :] = scale
        inverse = 1.0 / scale

        def step(i, carry):
            span = pl.ds(pl.multiple_of(i * BLOCK, BLOCK), BLOCK)
            out = pl.ds(pl.multiple_of(me * rows + i * BLOCK, BLOCK), BLOCK)
            finals[a][out, cols] = (held[a][span, cols] * inverse).astype(jnp.bfloat16)
            return carry

        lax.fori_loop(0, rows // BLOCK, step, 0)
        for k in range(n - 1):
            block_copy(c, k, me).start()

    combine(0)
    for c in range(len(chunks)):
        if c + 1 < len(chunks):
            combine(c + 1)
        finish(c)
    for c in range(len(chunks)):
        for k in range(n - 1):
            peak_copy(c, k, me).wait_send()
            block_copy(c, k, me).wait_send()
            block_copy(c, k, peers[k]).wait_recv()


def write_out(*refs):
    half = (len(refs) - 1) // 2
    sem = refs[-1]
    copies = [
        pltpu.make_async_copy(refs[i], refs[half + i], sem.at[i]) for i in range(half)
    ]
    for copy in copies:
        copy.start()
    for copy in copies:
        copy.wait()


def shards(
    n, one_query, other_query, one_key, other_key, one_value, other_value, mix_share, norm_gain
):
    ones = (one_query, one_key, one_value)
    others = (other_query, other_key, other_value)
    rows = one_query.shape[0]
    chunks = [(a, col) for a in range(3) for col in range(0, ones[a].shape[1], WIDTH)]
    count = len(chunks)
    vmem = pl.BlockSpec(memory_space=pltpu.VMEM)
    hbm = pl.BlockSpec(memory_space=pltpu.HBM)
    shapes = [((n * rows, x.shape[1]), jnp.bfloat16) for x in ones] + [
        ((x.shape[1] // LANES, LANES), jnp.float32) for x in ones
    ]
    scratch = (
        [pltpu.VMEM(x.shape, jnp.float32) for x in ones + others]
        + [pltpu.VMEM((rows // LANES, LANES), jnp.float32)] * 2
        + [pltpu.VMEM((rows, LANES), jnp.float32)] * 2
        + [
            pltpu.VMEM((count, n, 8, WIDTH), jnp.float32),
            pltpu.SemaphoreType.DMA((2,)),
            pltpu.SemaphoreType.DMA((count, 2)),
            pltpu.SemaphoreType.DMA((count, n - 1)),
            pltpu.SemaphoreType.DMA((count, n)),
            pltpu.SemaphoreType.DMA((count, n - 1)),
            pltpu.SemaphoreType.DMA((count, n)),
        ]
    )
    grant = sum(2 * x.size * 4 for x in ones) + 2 * rows * LANES * 4
    grant += count * n * 8 * WIDTH * 4 + (2 << 20)
    merged = pl.pallas_call(
        functools.partial(merge, n, chunks),
        out_shape=[pltpu.VMEM(s, d) for s, d in shapes],
        in_specs=[hbm] * 8,
        out_specs=[vmem] * 6,
        scratch_shapes=scratch,
        compiler_params=pltpu.CompilerParams(
            collective_id=0, has_side_effects=True, vmem_limit_bytes=grant
        ),
        name="merge",
    )(
        *(
            pltpu.with_memory_space_constraint(x, pltpu.HBM)
            for x in (
                *ones,
                *others,
                mix_share.reshape(rows // LANES, LANES),
                norm_gain.reshape(rows // LANES, LANES),
            )
        )
    )
    outs = pl.pallas_call(
        write_out,
        out_shape=[jax.ShapeDtypeStruct(s, d) for s, d in shapes],
        in_specs=[vmem] * 6,
        out_specs=[hbm] * 6,
        scratch_shapes=[pltpu.SemaphoreType.DMA((6,))],
        compiler_params=pltpu.CompilerParams(vmem_limit_bytes=1 << 20),
        name="write_out",
    )(*merged)
    return (*outs[:3], *(x.reshape(-1) for x in outs[3:]))


def solution(mesh):
    rows = P(("job", "shard"))
    blocks = P(("job", "shard"), "cols")
    return jax.shard_map(
        functools.partial(shards, mesh.shape["shard"]),
        mesh=mesh,
        in_specs=(blocks,) * 6 + (rows,) * 2,
        out_specs=(P("job", "cols"),) * 3 + (P(("job", "cols")),) * 3,
        check_vma=False,
    )
```

time: 94.4 us -> 28.7 us (0.30); the launches traced: 93.3 us -> 28.6 us
  waiting for transfers between devices: 41 us -> 0 us
  Pallas kernels: 0 us -> 28 us
  other arithmetic: 23.5 us -> 0 us
  between operations: 13.8 us -> 0.64 us
  local copies, waits for them, and re-layouts: 12.2 us -> 0 us
  blocking collectives: 2.79 us -> 0 us
    all_gather x3 -> x0, waiting for transfers between devices: 40.9 us -> none  [the longest x1 22.6 us: shards(): lax.all_gather(narrow_query, 'shard', axis=0, tiled=True)]
    pallas_call x0 -> x2, Pallas kernels: none -> 28 us  [the longest x1 23.2 us: shards(): pl.pallas_call(functools.partial(merge, n, chunks), out_shape=[pltpu.VMEM...]
    reduce_max x2 -> x0, other arithmetic: 12.3 us -> none  [the longest x1 10.3 us: shards(): jnp.max(jnp.abs(result_gained_query), axis=0)]
    unnamed x25 -> x0, local copies, waits for them, and re-layouts: 12.2 us -> none
    convert_element_type x3 -> x0, other arithmetic: 10.5 us -> none  [the longest x1 6.62 us: shards(): (result_gained_query / scale_query).astype(jnp.bfloat16)]
    pmax x1 -> x0, blocking collectives: 2.79 us -> none  [shards(): lax.pmax((jnp.max(jnp.abs(result_gained_query), axis=0), jnp.max(jnp.abs(...]
  transfers between devices with their start and end apart: 3 -> 0, of which waited for: 3 -> 0; matrix products, arithmetic and copies ran while one was open for 8% -> 0% of each run, Pallas kernels for 0% -> 0%
where the time goes in v1:
time: 28.7 us; the launch traced here: 28.6 us
  Pallas kernels  28 us (98%)
  between operations  0.64 us (2%)
    pallas_call x1, Pallas kernels, shards(): pl.pallas_call(functools.partial(merge, n, chunks), out_shape=[pltpu.VMEM...  23.2 us
    pallas_call x1, Pallas kernels, shards(): pl.pallas_call(write_out, out_shape=[jax.ShapeDtypeStruct(s, d) for s, d...  4.77 us

profile of v1, /device:TPU:3, one launch (start us, length us, event | category | flops | bytes accessed | tf_op | source)
XLA Modules:
  0.0 28.6 jit_solution(14931217103232816852)
XLA Ops:
  0.6 23.2 %merge.1 = (bf16[4096,1024]{1,0:T(8,128)(2,1)S(1)}, bf16[4096,256]{1,0:T(8,128)(2,1)S(1)}, bf16[4096,256]{1,0:T(8,128)(2,1)S(1)}, f32[8,128]{1,0:T(8,128)S(1)}, ...) custom-call(f32[2048,1024]{1,0:T(8,128)} %refs_0_.1, f32[2048,256]{1,0:T(8,128)} %refs_1_.1, f32[2048,256]{1,0:T(8,128)} %refs_2_.1, ...), custom_call_target="tpu_custom_call" | custom-call | tf_op jit(solution)/shard_map/merge/pallas_call | solution.py:174
  23.8 4.8 %write_out.1 = (bf16[4096,1024]{1,0:T(8,128)(2,1)}, bf16[4096,256]{1,0:T(8,128)(2,1)}, bf16[4096,256]{1,0:T(8,128)(2,1)}, f32[8,128]{1,0:T(8,128)}, f32[2,128]{1,0:T(2,128)}, /*index=5*/f32[2,128]{1,0:T(2,128)}) custom-call(bf16[4096,1024]{1,0:T(8,128)(2,1)S(1)} %get-tuple-element.18.refs_0_, bf16[4096,256]{1,0:T(8,128)(2,1)S(1)} %get-tuple-element.19.refs_1_, ...), custom_call_target="tpu_custom_call" | custom-call | tf_op jit(solution)/shard_map/write_out/pallas_call | solution.py:195

commit v2 on v1

--- a/solution.py
+++ b/solution.py
@@ -8,8 +8,9 @@
 from jax.sharding import PartitionSpec as P
 
 LANES = 128
-WIDTH = 128
-BLOCK = 128
+NARROW = 2
+WIDTH = 256
+BLOCK = 512
 MESH = pl.DeviceIdType.MESH
 
 
@@ -25,17 +26,18 @@
     peers = [lax.rem(me + k, n) for k in range(1, n)]
 
     def loads(c):
-        a, col = chunks[c]
-        cols = pl.ds(col, WIDTH)
+        a, col, width = chunks[c]
+        cols = pl.ds(col, width)
         return (
             pltpu.make_async_copy(ones[a].at[:, cols], held[a].at[:, cols], in_sem.at[c, 0]),
             pltpu.make_async_copy(others[a].at[:, cols], extra[a].at[:, cols], in_sem.at[c, 1]),
         )
 
     def peak_copy(c, k, slot):
+        width = chunks[c][2]
         return pltpu.make_async_remote_copy(
-            src_ref=peaks.at[c, slot],
-            dst_ref=peaks.at[c, slot],
+            src_ref=peaks.at[c, slot, :, pl.ds(0, width)],
+            dst_ref=peaks.at[c, slot, :, pl.ds(0, width)],
             send_sem=peak_send.at[c, k],
             recv_sem=peak_recv.at[c, slot],
             device_id={"shard": peers[k]},
@@ -43,8 +45,8 @@
         )
 
     def block_copy(c, k, slot):
-        a, col = chunks[c]
-        block = finals[a].at[pl.ds(pl.multiple_of(slot * rows, rows), rows), pl.ds(col, WIDTH)]
+        a, col, width = chunks[c]
+        block = finals[a].at[pl.ds(pl.multiple_of(slot * rows, rows), rows), pl.ds(col, width)]
         return pltpu.make_async_remote_copy(
             src_ref=block,
             dst_ref=block,
@@ -62,7 +64,7 @@
         copy.start()
     for c in range(len(chunks)):
         for copy in loads(c):
-            copy.start()
+            copy.start(priority=1)
 
     barrier = pltpu.get_barrier_semaphore()
     for peer in peers:
@@ -80,32 +82,42 @@
     pl.semaphore_wait(barrier, n - 1)
 
     def combine(c):
-        a, col = chunks[c]
+        a, col, width = chunks[c]
         for copy in loads(c):
             copy.wait()
-        cols = pl.ds(col, WIDTH)
+        lanes = range(0, width, LANES)
 
         def step(i, peak):
             span = pl.ds(pl.multiple_of(i * BLOCK, BLOCK), BLOCK)
-            value = first[span, :] * held[a][span, cols] + second[span, :] * extra[a][span, cols]
-            held[a][span, cols] = value
-            return jnp.maximum(peak, jnp.max(jnp.abs(value).reshape(BLOCK // 8, 8, WIDTH), axis=0))
-
-        peaks[c, me] = lax.fori_loop(0, rows // BLOCK, step, jnp.zeros((8, WIDTH), jnp.float32))
+            one_factor, other_factor = first[span, :], second[span, :]
+            tops = []
+            for j, top in zip(lanes, peak):
+                cols = pl.ds(col + j, LANES)
+                value = one_factor * held[a][span, cols] + other_factor * extra[a][span, cols]
+                held[a][span, cols] = value
+                top_here = jnp.max(jnp.abs(value).reshape(BLOCK // 8, 8, LANES), axis=0)
+                tops.append(jnp.maximum(top, top_here))
+            return tuple(tops)
+
+        zero = jnp.zeros((8, LANES), jnp.float32)
+        tops = lax.fori_loop(0, rows // BLOCK, step, (zero,) * len(lanes))
+        for j, top in zip(lanes, tops):
+            peaks[c, me, :, j : j + LANES] = top
         for k in range(n - 1):
             peak_copy(c, k, me).start()
 
     def finish(c):
-        a, col = chunks[c]
-        cols = pl.ds(col, WIDTH)
+        a, col, width = chunks[c]
+        cols = pl.ds(col, width)
         for k in range(n - 1):
             peak_copy(c, k, peers[k]).wait_recv()
-        peak = peaks[c, 0]
+        peak = peaks[c, 0, :, :width]
         for k in range(1, n):
-            peak = jnp.maximum(peak, peaks[c, k])
+            peak = jnp.maximum(peak, peaks[c, k, :, :width])
         scale = jnp.max(peak, axis=0, keepdims=True)
-        row = col // LANES
-        scales[a][row : row + 1, :] = scale
+        for j in range(0, width, LANES):
+            row = (col + j) // LANES
+            scales[a][row : row + 1, :] = scale[:, j : j + LANES]
         inverse = 1.0 / scale
 
         def step(i, carry):
@@ -142,13 +154,24 @@
         copy.wait()
 
 
+def cut(widths):
+    chunks = []
+    for a, total in enumerate(widths):
+        col = 0
+        while col < total:
+            width = min(LANES if len(chunks) < NARROW else WIDTH, total - col)
+            chunks.append((a, col, width))
+            col += width
+    return chunks
+
+
 def shards(
     n, one_query, other_query, one_key, other_key, one_value, other_value, mix_share, norm_gain
 ):
     ones = (one_query, one_key, one_value)
     others = (other_query, other_key, other_value)
     rows = one_query.shape[0]
-    chunks = [(a, col) for a in range(3) for col in range(0, ones[a].shape[1], WIDTH)]
+    chunks = cut([x.shape[1] for x in ones])
     count = len(chunks)
     vmem = pl.BlockSpec(memory_space=pltpu.VMEM)
     hbm = pl.BlockSpec(memory_space=pltpu.HBM)

time: 28.7 us -> 20.4 us (0.71)
  Pallas kernels: 28 us -> 19.6 us
    pallas_call x1, Pallas kernels: 23.2 us -> 14.8 us  [shards(): pl.pallas_call(functools.partial(merge, n, chunks), out_shape=[pltpu.VMEM...]
where the time goes in v2:
time: 20.4 us; the launch traced here: 20.2 us
  Pallas kernels  19.6 us (96%)
  between operations  0.64 us (3%)
    pallas_call x1, Pallas kernels, shards(): pl.pallas_call(functools.partial(merge, n, chunks), out_shape=[pltpu.VMEM...  14.8 us
    pallas_call x1, Pallas kernels, shards(): pl.pallas_call(write_out, out_shape=[jax.ShapeDtypeStruct(s, d) for s, d...  4.77 us

profile of v2, /device:TPU:3, one launch (start us, length us, event | category | flops | bytes accessed | tf_op | source)
XLA Modules:
  0.0 20.2 jit_solution(4689580894213718118)
XLA Ops:
  0.6 14.8 %merge.1 = (bf16[4096,1024]{1,0:T(8,128)(2,1)S(1)}, bf16[4096,256]{1,0:T(8,128)(2,1)S(1)}, bf16[4096,256]{1,0:T(8,128)(2,1)S(1)}, f32[8,128]{1,0:T(8,128)S(1)}, ...) custom-call(f32[2048,1024]{1,0:T(8,128)} %refs_0_.1, f32[2048,256]{1,0:T(8,128)} %refs_1_.1, f32[2048,256]{1,0:T(8,128)} %refs_2_.1, ...), custom_call_target="tpu_custom_call" | custom-call | tf_op jit(solution)/shard_map/merge/pallas_call | solution.py:197
  15.4 4.8 %write_out.1 = (bf16[4096,1024]{1,0:T(8,128)(2,1)}, bf16[4096,256]{1,0:T(8,128)(2,1)}, bf16[4096,256]{1,0:T(8,128)(2,1)}, f32[8,128]{1,0:T(8,128)}, f32[2,128]{1,0:T(2,128)}, /*index=5*/f32[2,128]{1,0:T(2,128)}) custom-call(bf16[4096,1024]{1,0:T(8,128)(2,1)S(1)} %get-tuple-element.18.refs_0_, bf16[4096,256]{1,0:T(8,128)(2,1)S(1)} %get-tuple-element.19.refs_1_, ...), custom_call_target="tpu_custom_call" | custom-call | tf_op jit(solution)/shard_map/write_out/pallas_call | solution.py:218
